TPU v7x, 32 devices: a whole 2x2x4 slice. The times are simulated.
32 devices in a mesh: dp: 8 (over y, x, core), tensor: 4 (over z).
Axes of the slice: x: 2, y: 2, z: 4, core: 2. Of those that a mesh axis runs over, the one named last changes fastest.
Arguments:
- inputs: bfloat16 [12288, 768], P(('dp', 'tensor')), may hold values from -6 to 6
- segments: int32 [24, 512], P('dp'), may hold values from 0 to 3, never falling along the last dimension, each value on 1 to 256 neighbouring positions
- labels: int32 [24], P('dp'), may hold values from 0 to 2
- qkv_weight: bfloat16 [3, 768, 768], P(None, None, 'tensor'), may hold values from -0.21875 to 0.21875
- qv_bias: float32 [2, 768], P(None, 'tensor'), may hold values from -3 to 3
- out_weight: bfloat16 [768, 768], P('tensor'), may hold values from -0.875 to 0.875
- out_bias: float32 [768], replicated, may hold values from -3 to 3
- norm1_gain: float32 [768], replicated, may hold values from 0.5 to 1.5
- norm1_bias: float32 [768], replicated, may hold values from -3 to 3
- up_weight: bfloat16 [768, 3072], P(None, 'tensor'), may hold values from -0.21875 to 0.21875
- up_bias: float32 [3072], P('tensor'), may hold values from -3 to 3
- down_weight: bfloat16 [3072, 768], P('tensor'), may hold values from -0.109375 to 0.109375
- down_bias: float32 [768], replicated, may hold values from -3 to 3
- norm2_gain: float32 [768], replicated, may hold values from 0.5 to 1.5
- norm2_bias: float32 [768], replicated, may hold values from -3 to 3
- pool_weight: bfloat16 [768, 768], replicated, may hold values from -0.21875 to 0.21875
- pool_bias: float32 [768], replicated, may hold values from -3 to 3
- class_weight: bfloat16 [768, 3], replicated, may hold values from -0.4375 to 0.4375
- class_bias: float32 [3], replicated, may hold values from -4 to 4
- cotangent: bfloat16 [12288, 768], P(('dp', 'tensor')), may hold values from -6 to 6
Outputs:
- hidden: bfloat16 [12288, 768], P(('dp', 'tensor'))
- input_grad: bfloat16 [12288, 768], P(('dp', 'tensor'))
- qkv_weight_grad: float32 [3, 768, 768], P(None, 'dp', 'tensor')
- qv_bias_grad: float32 [2, 768], P(None, 'tensor')
- out_weight_grad: float32 [768, 768], P('tensor', 'dp')
- out_bias_grad: float32 [768], replicated
- norm1_gain_grad: float32 [768], replicated
- norm1_bias_grad: float32 [768], replicated
- up_weight_grad: float32 [768, 3072], P('dp', 'tensor')
- up_bias_grad: float32 [3072], P('tensor')
- down_weight_grad: float32 [3072, 768], P('tensor', 'dp')
- down_bias_grad: float32 [768], replicated
- norm2_gain_grad: float32 [768], replicated
- norm2_bias_grad: float32 [768], replicated
- pool_weight_grad: float32 [768, 768], replicated
- pool_bias_grad: float32 [768], replicated
- class_weight_grad: float32 [768, 3], replicated
- class_bias_grad: float32 [3], replicated
Inputs may be any that keep to these rules, and one draw needn't show every extreme that they name: `segments`: along each packed row of 512 tokens the ids never fall; a document holds at most half of 512 tokens.
All inputs are finite; a program needn't handle non-finite values.
Results may differ from a plain program's by a relative error of at most 0.017.
The roundings to bfloat16 on the way count: a program that leaves them out, or rounds other values in their place, can miss the bound.
Values may be sent and summed in bfloat16 or wider, within the bound.
A program may use at most 128 MiB of HBM per device.

v0:
```python
from functools import partial
import jax
import jax.numpy as jnp
from jax import lax
from jax.sharding import PartitionSpec as P

HEAD = 64
epsilon = 1e-12
masked_value = -1e30


def norm_forward(values, norm_gain, norm_shift):
    centre = values - jnp.mean(values, axis=-1, keepdims=True)
    inverse = lax.rsqrt(jnp.mean(centre * centre, axis=-1, keepdims=True) + epsilon)
    normed = centre * inverse
    return (normed * norm_gain + norm_shift, normed, inverse)


def norm_backward(grad_out, normed, inverse, norm_gain):
    scaled = grad_out * norm_gain
    grad_in = inverse * (
        scaled
        - jnp.mean(scaled, axis=-1, keepdims=True)
        - normed * jnp.mean(scaled * normed, axis=-1, keepdims=True)
    )
    return (grad_in, jnp.sum(grad_out * normed, axis=0), jnp.sum(grad_out, axis=0))


def split_heads(rows):
    return rows.reshape(rows.shape[0], rows.shape[1] // HEAD, HEAD)


def masked_scores(query_heads, key_heads, segment_row):
    raw_scores = jnp.einsum(
        "qhe,khe->hqk", query_heads, key_heads, preferred_element_type=jnp.float32
    ) * HEAD ** (-0.5)
    allowed = segment_row[:, None] == segment_row[None, :]
    return (jnp.where(allowed[None], raw_scores, masked_value), allowed)


def attend_sequence(block_items):
    query_seq, key_seq, value_seq, segment_row = block_items
    scores, allowed = masked_scores(split_heads(query_seq), split_heads(key_seq), segment_row)
    largest = jnp.max(scores, axis=-1, keepdims=True)
    exponent = jnp.exp(scores - largest)
    row_total = jnp.sum(exponent, axis=-1, keepdims=True)
    soft_low = (exponent / row_total).astype(jnp.bfloat16)
    context = jnp.einsum(
        "hqk,khe->qhe", soft_low, split_heads(value_seq), preferred_element_type=jnp.float32
    )
    context = context.reshape(query_seq.shape).astype(jnp.bfloat16)
    return (context, largest[..., 0] + jnp.log(row_total[..., 0]))


def attend_backward(block_items):
    query_seq, key_seq, value_seq, segment_row, log_total, grad_context = block_items
    query_heads = split_heads(query_seq)
    key_heads = split_heads(key_seq)
    value_heads = split_heads(value_seq)
    grad_heads = split_heads(grad_context)
    scores, allowed = masked_scores(query_heads, key_heads, segment_row)
    soft_probs = jnp.exp(scores - log_total[..., None])
    grad_values = jnp.einsum(
        "hqk,qhe->khe",
        soft_probs.astype(jnp.bfloat16),
        grad_heads,
        preferred_element_type=jnp.float32,
    )
    grad_soft = jnp.einsum(
        "qhe,khe->hqk", grad_heads, value_heads, preferred_element_type=jnp.float32
    )
    grad_scores = soft_probs * (grad_soft - jnp.sum(soft_probs * grad_soft, axis=-1, keepdims=True))
    grad_low = jnp.where(allowed[None], grad_scores, 0.0).astype(jnp.bfloat16)
    score_scale = HEAD ** (-0.5)
    grad_queries = (
        jnp.einsum("hqk,khe->qhe", grad_low, key_heads, preferred_element_type=jnp.float32)
        * score_scale
    )
    grad_keys = (
        jnp.einsum("hqk,qhe->khe", grad_low, query_heads, preferred_element_type=jnp.float32)
        * score_scale
    )
    full_shape = query_seq.shape
    return (
        grad_queries.reshape(full_shape).astype(jnp.bfloat16),
        grad_keys.reshape(full_shape).astype(jnp.bfloat16),
        grad_values.reshape(full_shape).astype(jnp.bfloat16),
    )


def body(
    inputs,
    segments,
    labels,
    qkv_weight,
    qv_bias,
    out_weight,
    out_bias,
    norm1_gain,
    norm1_bias,
    up_weight,
    up_bias,
    down_weight,
    down_bias,
    norm2_gain,
    norm2_bias,
    pool_weight,
    pool_bias,
    class_weight,
    class_bias,
    cotangent,
):
    share_rows = inputs.shape[0]
    seq_count, seq_length = segments.shape
    offset = lax.axis_index("tensor") * share_rows

    def take_share(array):
        return lax.dynamic_slice_in_dim(array, offset, share_rows, 0)

    gathered = lax.all_gather(inputs, "tensor", axis=0, tiled=True)
    group_rows = gathered.shape[0]
    projected = jnp.einsum("td,kde->kte", gathered, qkv_weight, preferred_element_type=jnp.float32)
    queries = (projected[0] + qv_bias[0]).astype(jnp.bfloat16)
    key_rows = projected[1].astype(jnp.bfloat16)
    value_rows = (projected[2] + qv_bias[1]).astype(jnp.bfloat16)
    local_width = queries.shape[1]

    def by_sequence(rows):
        return rows.reshape(seq_count, seq_length, rows.shape[-1])

    context, log_totals = lax.map(
        attend_sequence,
        (by_sequence(queries), by_sequence(key_rows), by_sequence(value_rows), segments),
    )
    context = context.reshape(group_rows, local_width)
    attended_all = (
        lax.psum(jnp.dot(context, out_weight, preferred_element_type=jnp.float32), "tensor")
        + out_bias
    )
    first_whole, normed_whole, inverse_whole = norm_forward(
        gathered.astype(jnp.float32) + attended_all, norm1_gain, norm1_bias
    )
    first_all = first_whole.astype(jnp.bfloat16)
    normed_one = take_share(normed_whole)
    inverse_one = take_share(inverse_whole)
    up_pre = jnp.dot(first_all, up_weight, preferred_element_type=jnp.float32) + up_bias
    gelu_exact = partial(jax.nn.gelu, approximate=False)
    active = gelu_exact(up_pre).astype(jnp.bfloat16)
    ffn_all = (
        lax.psum(jnp.dot(active, down_weight, preferred_element_type=jnp.float32), "tensor")
        + down_bias
    )
    final_whole, normed_all, inverse_all = norm_forward(
        first_whole + ffn_all, norm2_gain, norm2_bias
    )
    final_norm = take_share(final_whole)
    normed_two = take_share(normed_all)
    inverse_two = take_share(inverse_all)
    positions = offset + jnp.arange(share_rows, dtype=jnp.int32)
    row_starts = jnp.arange(seq_count, dtype=jnp.int32) * seq_length
    selector = (row_starts[:, None] == positions[None, :]).astype(jnp.float32)
    leading_part = jnp.dot(selector, final_norm, precision=lax.Precision.HIGHEST)
    leading = lax.psum(leading_part, "tensor").astype(jnp.bfloat16)
    pooled = jnp.tanh(jnp.dot(leading, pool_weight, preferred_element_type=jnp.float32) + pool_bias)
    pooled_low = pooled.astype(jnp.bfloat16)
    logits = jnp.dot(pooled_low, class_weight, preferred_element_type=jnp.float32) + class_bias
    chosen = (
        labels[:, None] == jnp.arange(class_weight.shape[1], dtype=jnp.int32)[None, :]
    ).astype(jnp.float32)
    grad_logits = (jax.nn.softmax(logits, axis=-1) - chosen).astype(jnp.bfloat16)
    class_weight_grad = jnp.einsum(
        "rd,rc->dc", pooled_low, grad_logits, preferred_element_type=jnp.float32
    )
    class_bias_grad = jnp.sum(grad_logits.astype(jnp.float32), axis=0)
    grad_pre = (
        jnp.einsum("rc,dc->rd", grad_logits, class_weight, preferred_element_type=jnp.float32)
        * (1.0 - pooled * pooled)
    ).astype(jnp.bfloat16)
    pool_weight_grad = jnp.einsum(
        "rd,re->de", leading, grad_pre, preferred_element_type=jnp.float32
    )
    pool_bias_grad = jnp.sum(grad_pre.astype(jnp.float32), axis=0)
    grad_leading = jnp.einsum(
        "re,de->rd", grad_pre, pool_weight, preferred_element_type=jnp.float32
    )
    grad_final = cotangent.astype(jnp.float32) + jnp.einsum(
        "rt,rd->td", selector, grad_leading, precision=lax.Precision.HIGHEST
    )
    grad_second, norm2_gain_grad, norm2_bias_grad = norm_backward(
        grad_final, normed_two, inverse_two, norm2_gain
    )
    grad_fed = grad_second.astype(jnp.bfloat16)
    down_bias_grad = jnp.sum(grad_fed.astype(jnp.float32), axis=0)
    grad_fed_all = lax.all_gather(grad_fed, "tensor", axis=0, tiled=True)
    down_weight_grad = jnp.einsum(
        "tf,td->fd", active, grad_fed_all, preferred_element_type=jnp.float32
    )
    grad_active = jnp.einsum(
        "td,fd->tf", grad_fed_all, down_weight, preferred_element_type=jnp.float32
    )
    grad_up = jax.vjp(gelu_exact, up_pre)[1](grad_active)[0].astype(jnp.bfloat16)
    up_bias_grad = jnp.sum(grad_up.astype(jnp.float32), axis=0)
    up_weight_grad = jnp.einsum("td,tf->df", first_all, grad_up, preferred_element_type=jnp.float32)
    grad_first = (
        lax.psum_scatter(
            jnp.einsum("tf,df->td", grad_up, up_weight, preferred_element_type=jnp.float32),
            "tensor",
            scatter_dimension=0,
            tiled=True,
        )
        + grad_second
    )
    grad_res, norm1_gain_grad, norm1_bias_grad = norm_backward(
        grad_first, normed_one, inverse_one, norm1_gain
    )
    grad_att = grad_res.astype(jnp.bfloat16)
    out_bias_grad = jnp.sum(grad_att.astype(jnp.float32), axis=0)
    grad_att_all = lax.all_gather(grad_att, "tensor", axis=0, tiled=True)
    out_weight_grad = jnp.einsum(
        "te,td->ed", context, grad_att_all, preferred_element_type=jnp.float32
    )
    grad_context = jnp.einsum(
        "td,ed->te", grad_att_all, out_weight, preferred_element_type=jnp.float32
    ).astype(jnp.bfloat16)
    grad_queries, grad_keys, grad_values = lax.map(
        attend_backward,
        (
            by_sequence(queries),
            by_sequence(key_rows),
            by_sequence(value_rows),
            segments,
            log_totals,
            by_sequence(grad_context),
        ),
    )
    stacked = jnp.stack(
        [
            grad_queries.reshape(group_rows, local_width),
            grad_keys.reshape(group_rows, local_width),
            grad_values.reshape(group_rows, local_width),
        ]
    )
    qkv_weight_grad = jnp.einsum(
        "td,kte->kde", gathered, stacked, preferred_element_type=jnp.float32
    )
    qv_bias_grad = jnp.stack(
        [
            jnp.sum(stacked[0].astype(jnp.float32), axis=0),
            jnp.sum(stacked[2].astype(jnp.float32), axis=0),
        ]
    )
    input_grad = (
        lax.psum_scatter(
            jnp.einsum(
                "kte,kde->td", stacked, qkv_weight, preferred_element_type=jnp.float32
            ).astype(jnp.bfloat16),
            "tensor",
            scatter_dimension=0,
            tiled=True,
        ).astype(jnp.float32)
        + grad_res
    ).astype(jnp.bfloat16)
    qkv_sum, out_sum, up_sum, down_sum = (
        lax.psum_scatter(qkv_weight_grad, "dp", scatter_dimension=1, tiled=True),
        lax.psum_scatter(out_weight_grad, "dp", scatter_dimension=1, tiled=True),
        lax.psum_scatter(up_weight_grad, "dp", scatter_dimension=0, tiled=True),
        lax.psum_scatter(down_weight_grad, "dp", scatter_dimension=1, tiled=True),
    )
    token_grads = lax.psum(
        (
            out_bias_grad,
            norm1_gain_grad,
            norm1_bias_grad,
            down_bias_grad,
            norm2_gain_grad,
            norm2_bias_grad,
        ),
        ("dp", "tensor"),
    )
    group_grads = lax.psum(
        (
            qv_bias_grad,
            up_bias_grad,
            pool_weight_grad,
            pool_bias_grad,
            class_weight_grad,
            class_bias_grad,
        ),
        "dp",
    )
    return (
        final_norm.astype(jnp.bfloat16),
        input_grad,
        qkv_sum,
        group_grads[0],
        out_sum,
        token_grads[0],
        token_grads[1],
        token_grads[2],
        up_sum,
        group_grads[1],
        down_sum,
        token_grads[3],
        token_grads[4],
        token_grads[5],
        group_grads[2],
        group_grads[3],
        group_grads[4],
        group_grads[5],
    )


def solution(mesh):
    placed = (
        P(("dp", "tensor"), None),
        P("dp", None),
        P("dp"),
        P(None, None, "tensor"),
        P(None, "tensor"),
        P("tensor", None),
        P(),
        P(),
        P(),
        P(None, "tensor"),
        P("tensor"),
        P("tensor", None),
        P(),
        P(),
        P(),
        P(),
        P(),
        P(),
        P(),
        P(("dp", "tensor"), None),
    )
    return jax.shard_map(
        body,
        mesh=mesh,
        in_specs=placed,
        out_specs=(
            P(("dp", "tensor"), None),
            P(("dp", "tensor"), None),
            P(None, "dp", "tensor"),
            P(None, "tensor"),
            P("tensor", "dp"),
            P(),
            P(),
            P(),
            P("dp", "tensor"),
            P("tensor"),
            P("tensor", "dp"),
            P(),
            P(),
            P(),
            P(),
            P(),
            P(),
            P(),
        ),
        check_vma=False,
    )
```

profile of v0, /device:TPU:0, one launch (start us, length us, event | category | flops | bytes accessed | tf_op | source)
XLA Modules:
  0.0 1093.7 jit_solution(14431650405853245202)
XLA Ops:
  8.8 53.6 %all-gather.4.cloned.1.call-done = bf16[1536,768]{1,0:T(8,128)(2,1)} async-done(((bf16[384,768]{1,0:T(8,128)(2,1)}), bf16[1536,768]{1,0:T(8,128)(2,1)}) %all-gather.4.cloned.1.call-update) | async-done | bytes 2359312 | tf_op jit(solution)/shard_map/all_gather | solution.py:120
  62.3 3.5 convolution_bitcast_fusion
  65.8 1.5 fusion.88
  68.3 1.9 squeeze.20
  70.7 1.9 squeeze.21
  73.1 2.1 convert_element_type.164
  76.6 12.6 %while.26 = (s32[]{:T(128)}, bf16[3,512,192]{1,2,0:T(8,128)(2,1)S(1)}, f32[3,3,512]{2,1,0:T(4,128)}, bf16[3,512,192]{1,2,0:T(8,128)(2,1)S(1)}, s32[3,512]{1,0:T(...) while((s32[]{:T(128)}, bf16[3,512,192]{1,2,0:T(8,128)(2,1)S(1)}, ...), condition=%wide.region_3.4_spmd, body=%wide.region_0.3_spmd.sunk | while | flops 211122688 | bytes 12902513 | solution.py:131
  90.5 4.0 fusion.92
  94.9 170.5 %all-reduce.6.cloned.1.call-done = f32[1536,768]{1,0:T(8,128)} async-done(((f32[1536,768]{1,0:T(8,128)}), f32[1536,768]{1,0:T(8,128)}) %all-reduce.6.cloned.1.call-update) | async-done | bytes 4718608 | tf_op jit(solution)/shard_map/psum | solution.py:137
  265.4 3.2 fusion.52
  272.2 13.3 %multiply_convert_fusion = (bf16[1536,768]{1,0:T(8,128)(2,1)S(1)}, f32[1536,768]{1,0:T(8,128)}, f32[1536,768]{1,0:T(8,128)}) fusion(f32[768]{0:T(1024)S(1)} %copy-done.40, bf16[768,768]{1,0:T(8,128)(2,1)S(1)} %copy-done, f32[1536,768]{1,0:T(8,128)S(1)} %subtract_multiply_fusion.1, f32[768]{0:T(1024)S(1)} %copy-done.35, f32[768]{0:T(1024)S(1)} %copy-done.22), kind=kOutput, calls=%fused_computation.53 | convolution fusion | flops 1893335040 | bytes 17703936 | tf_op jit(solution)/shard_map/dot_general | solution.py:146
  286.9 4.2 fusion.93
  291.2 171.0 %all-reduce.8.cloned.1.call-done = f32[1536,768]{1,0:T(8,128)} async-done(((f32[1536,768]{1,0:T(8,128)}), f32[1536,768]{1,0:T(8,128)}) %all-reduce.8.cloned.1.call-update) | async-done | bytes 4718608 | tf_op jit(solution)/shard_map/psum | solution.py:150
  462.2 4.7 fusion.86
  468.2 2.0 copy-done.5
  470.8 16.4 %psum.107 = bf16[3,768]{1,0:T(4,128)(2,1)S(1)} all-reduce(f32[3,768]{1,0:T(4,128)S(1)} %fusion.56), channel_id=1, replica_groups=mesh['dp'=8,'tensor'=4] {'tensor'}, use_global_device_ids=true, to_apply=%region_10.11 | all-reduce | flops 2304 | bytes 13824 | tf_op jit(solution)/shard_map/psum | solution.py:163
  489.6 3.0 multiply_reduce_fusion.3
  492.6 3.0 convert_reduce_fusion.1
  496.2 47.9 %all-gather.6.cloned.1.call-done = bf16[1536,768]{1,0:T(8,128)(2,1)} async-done(((bf16[384,768]{1,0:T(8,128)(2,1)}), bf16[1536,768]{1,0:T(8,128)(2,1)}) %all-gather.6.cloned.1.call-update) | async-done | bytes 2359312 | tf_op jit(solution)/shard_map/all_gather | solution.py:194
  544.1 8.8 convert_reduce_fusion
  554.3 4.3 fusion.95
  559.5 83.4 %reduce-scatter.11.cloned.1.call-done = f32[384,768]{1,0:T(8,128)} async-done(((f32[1536,768]{1,0:T(8,128)}), f32[384,768]{1,0:T(8,128)}) %reduce-scatter.11.cloned.1.call-update) | async-done | bytes 1179664 | tf_op jit(solution)/shard_map/reduce_scatter | solution.py:205
  642.8 4.1 multiply_reduce_fusion.4
  648.0 3.0 convert_reduce_fusion.2
  651.2 50.4 %all-gather.8.cloned.1.call-done = bf16[1536,768]{1,0:T(8,128)(2,1)} async-done(((bf16[384,768]{1,0:T(8,128)(2,1)}), bf16[1536,768]{1,0:T(8,128)(2,1)}) %all-gather.8.cloned.1.call-update) | async-done | bytes 2359312 | tf_op jit(solution)/shard_map/all_gather | solution.py:218
  701.6 2.6 convolution_convert_fusion
  706.1 75.7 %while.27 = (s32[]{:T(128)}, bf16[3,512,192]{1,2,0:T(8,128)(2,1)S(1)}, bf16[3,512,192]{1,2,0:T(8,128)(2,1)}, bf16[3,512,192]{1,2,0:T(8,128)(2,1)S(1)}, bf16[3,51...) while((s32[]{:T(128)}, ...), condition=%wide.region_20.21_spmd, body=%wide.region_18.20_spmd.sunk | while | flops 515084288 | bytes 27811988 | solution.py:225
  709.6 2.6 subtract_exponential_fusion.4
  714.1 2.4 fusion.175
  716.5 5.8 fusion.176
  722.3 2.5 fusion.177
  724.8 5.8 fusion.178
  734.9 2.6 subtract_exponential_fusion.4
  739.4 2.4 fusion.175
  741.7 5.8 fusion.176
  747.5 2.5 fusion.177
  750.0 5.8 fusion.178
  760.1 2.6 subtract_exponential_fusion.4
  764.6 2.4 fusion.175
  767.0 5.8 fusion.176
  772.8 2.5 fusion.177
  775.3 5.8 fusion.178
  783.2 2.5 stack_reshape.9
  785.7 1.9 constant_dynamic-update-slice_fusion.6
  789.0 2.5 stack_reshape.10
  793.6 3.9 convolution_bitcast_fusion.1
  797.6 1.9 constant_dynamic-update-slice_fusion.5
  799.5 1.9 constant_dynamic-update-slice_fusion.4
  801.4 4.3 fusion.49
  805.7 4.2 copy.87
  809.9 4.8 reshape.315
  815.0 4.6 bitcast_convert_fusion
  819.7 2.0 fusion.97
  821.7 6.6 fusion.58
  828.5 5.9 fusion.96
  836.0 40.0 %all-reduce = (f32[768]{0:T(1024)}, f32[768]{0:T(1024)}, f32[768]{0:T(1024)}, f32[768]{0:T(1024)}, f32[768]{0:T(1024)}, /*index=5*/f32[768]{0:T(1024)}) all-reduce(f32[768]{0:T(1024)} %get-tuple-element.275, f32[768]{0:T(1024)} %get-tuple-element.222, ...), channel_id=1, replica_groups=mesh['dp'=8,'tensor'=4] {'dp','tensor'}, use_global_device_ids=true, to_apply=%region_28.29 | all-reduce | flops 4608 | bytes 36864 | tf_op jit(solution)/shard_map/psum | solution.py:269
  876.3 25.2 %all-reduce.1 = (f32[2,192]{1,0:T(2,128)}, f32[768]{0:T(1024)}, f32[768]{0:T(1024)}, f32[768,3]{0,1:T(4,128)}, f32[3]{0:T(128)}) all-reduce(f32[2,192]{1,0:T(2,128)S(1)} %pad_maximum_fusion, f32[768]{0:T(1024)} %get-tuple-element.279, f32[768]{0:T(1024)} %get-tuple-element.301, ...), channel_id=1, replica_groups=mesh['dp'=8,'tensor'=4] {'dp'}, use_global_device_ids=true, to_apply=%region_25.26 | all-reduce | flops 4227 | bytes 33816 | tf_op jit(solution)/shard_map/psum | solution.py:280
  901.5 1.6 copy.90
  905.0 21.0 %reduce-scatter.13.cloned.1.call-done = bf16[384,768]{1,0:T(8,128)(2,1)} async-done(((bf16[1536,768]{1,0:T(8,128)(2,1)}), bf16[384,768]{1,0:T(8,128)(2,1)}) %reduce-scatter.13.cloned.1.call-update) | async-done | bytes 589840 | tf_op jit(solution)/shard_map/reduce_scatter | solution.py:253
  926.1 2.6 add_convert_fusion.3
  928.7 62.9 %all-reduce.10.cloned.1.call-done = f32[768,768]{1,0:T(8,128)} async-done(((f32[768,768]{1,0:T(8,128)}), f32[768,768]{1,0:T(8,128)}) %all-reduce.10.cloned.1.call-update) | async-done | bytes 2359312 | tf_op jit(solution)/shard_map/psum | solution.py:280
  991.6 45.7 %reduce-scatter.15.cloned.1.call-done = f32[96,768]{1,0:T(8,128)} async-done(((f32[768,768]{1,0:T(8,128)}), f32[96,768]{1,0:T(8,128)}) %reduce-scatter.15.cloned.1.call-update) | async-done | bytes 294928 | tf_op jit(solution)/shard_map/reduce_scatter | solution.py:266
  1037.2 46.2 %reduce-scatter.17.cloned.1.call-done = f32[768,96]{0,1:T(8,128)} async-done(((f32[768,768]{0,1:T(8,128)}), f32[768,96]{0,1:T(8,128)}) %reduce-scatter.17.cloned.1.call-update) | async-done | bytes 294928 | tf_op jit(solution)/shard_map/reduce_scatter | solution.py:267
  1083.4 3.2 copy.129
  (215 shorter events, 61.4 us)
Async XLA Ops:
  7.2 265.0 %copy-start = (bf16[768,768]{1,0:T(8,128)(2,1)S(1)}, bf16[768,768]{1,0:T(8,128)(2,1)}, u32[]{:S(2)}) copy-start(bf16[768,768]{1,0:T(8,128)(2,1)} %param.33) | copy-start | bytes 3538948
  7.2 55.1 %all-gather.4.cloned.1.call-start = ((), (), s32[]{:S(2)}) async-start(), calls=%async_computation.6 | async-start | bytes 2949120 | tf_op jit(solution)/shard_map/all_gather | solution.py:120
  7.9 257.5 %all-reduce.6.cloned.1.call-start = ((), (), s32[]{:S(2)}) async-start(), calls=%async_computation.7 | async-start | bytes 9437184 | tf_op jit(solution)/shard_map/psum | solution.py:137
  89.2 0.8 copy-start.6
  89.2 1.0 copy-start.7
  89.2 1.2 copy-start.8
  89.2 1.3 copy-start.15
  94.5 170.9 %copy-start.3 = (bf16[1536,768]{1,0:T(8,128)(2,1)S(1)}, bf16[1536,768]{1,0:T(8,128)(2,1)}, u32[]{:S(2)}) copy-start(bf16[1536,768]{1,0:T(8,128)(2,1)} %all-gather.4.cloned.1.call-done) | copy-start | bytes 7077892
  94.5 170.9 %copy-start.26 = (f32[768]{0:T(1024)S(1)}, f32[768]{0:T(1024)}, u32[]{:S(2)}) copy-start(f32[768]{0:T(1024)} %param.30) | copy-start | bytes 9220
  94.5 367.7 %all-reduce.8.cloned.1.call-start = ((), (), s32[]{:S(2)}) async-start(), calls=%async_computation.8 | async-start | bytes 9437184 | tf_op jit(solution)/shard_map/psum | solution.py:150
  265.4 3.8 copy-start.1
  270.4 0.6 copy-start.25
  271.0 1.2 copy-start.22
  271.0 1.2 copy-start.35
  271.0 1.2 copy-start.40
  272.2 13.3 %copy-start.2 = (f32[1536,768]{1,0:T(8,128)}, f32[1536,768]{1,0:T(8,128)S(1)}, u32[]{:S(2)}) copy-start(f32[1536,768]{1,0:T(8,128)S(1)} %subtract_multiply_fusion.1) | copy-start | bytes 14155780
  272.2 14.7 %copy-start.38 = (bf16[768,768]{1,0:T(8,128)(2,1)S(1)}, bf16[768,768]{1,0:T(8,128)(2,1)}, u32[]{:S(2)}) copy-start(bf16[768,768]{1,0:T(8,128)(2,1)} %param.35) | copy-start | bytes 3538948
  285.5 1.4 copy-start.43
  291.1 171.1 %copy-start.33 = (f32[768]{0:T(1024)S(1)}, f32[768]{0:T(1024)}, u32[]{:S(2)}) copy-start(f32[768]{0:T(1024)} %param.36) | copy-start | bytes 9220
  291.1 253.0 %all-gather.6.cloned.1.call-start = ((), (), s32[]{:S(2)}) async-start(), calls=%async_computation.9 | async-start | bytes 2949120 | tf_op jit(solution)/shard_map/all_gather | solution.py:194
  467.5 2.7 copy-start.21
  467.6 2.7 copy-start.32
  467.6 19.7 %copy-start.16 = (bf16[768,768]{1,0:T(8,128)(2,1)S(1)}, bf16[768,768]{1,0:T(8,128)(2,1)}, u32[]{:S(2)}) copy-start(bf16[768,768]{1,0:T(8,128)(2,1)} %param.39) | copy-start | bytes 3538948
  467.6 19.7 %copy-start.34 = (f32[768]{0:T(1024)S(1)}, f32[768]{0:T(1024)}, u32[]{:S(2)}) copy-start(f32[768]{0:T(1024)} %param.40) | copy-start | bytes 9220
  467.6 19.9 %copy-start.39 = (bf16[768,3]{0,1:T(4,128)(2,1)S(1)}, bf16[768,3]{0,1:T(4,128)(2,1)}, u32[]{:S(2)}) copy-start(bf16[768,3]{0,1:T(4,128)(2,1)} %param.41) | copy-start | bytes 13828
  467.6 19.9 %copy-start.42 = (f32[3]{0:T(128)S(1)}, f32[3]{0:T(128)}, u32[]{:S(2)}) copy-start(f32[3]{0:T(128)} %param.42) | copy-start | bytes 40
  467.6 20.1 %copy-start.37 = (s32[3]{0:T(128)S(1)}, s32[3]{0:T(128)}, u32[]{:S(2)}) copy-start(s32[3]{0:T(128)} %param.26) | copy-start | bytes 40
  468.1 2.1 copy-start.5
  468.1 21.4 %copy-start.18 = (bf16[384,768]{1,0:T(8,128)(2,1)S(1)}, bf16[384,768]{1,0:T(8,128)(2,1)}, u32[]{:S(2)}) copy-start(bf16[384,768]{1,0:T(8,128)(2,1)} %param.43) | copy-start | bytes 1769476
  487.5 1.6 copy-start.23
  488.4 0.8 copy-start.36
  489.1 6.4 copy-start.27
  489.6 54.5 %copy-start.41 = (f32[768]{0:T(1024)S(1)}, f32[768]{0:T(1024)}, u32[]{:S(2)}) copy-start(f32[768]{0:T(1024)} %param.34) | copy-start | bytes 9220
  495.6 147.2 %reduce-scatter.11.cloned.1.call-start = ((), (), s32[]{:S(2)}) async-start(), calls=%async_computation.10 | async-start | bytes 5898240 | tf_op jit(solution)/shard_map/reduce_scatter | solution.py:205
  552.9 1.4 copy-start.44
  558.6 143.0 %all-gather.8.cloned.1.call-start = ((), (), s32[]{:S(2)}) async-start(), calls=%async_computation.11 | async-start | bytes 2949120 | tf_op jit(solution)/shard_map/all_gather | solution.py:218
  559.4 87.5 %copy-start.29 = (f32[384]{0:T(512)}, f32[384]{0:T(512)S(1)}, u32[]{:S(2)}) copy-start(f32[384]{0:T(512)S(1)} %dynamic-slice.6) | copy-start | bytes 4612
  646.9 1.0 copy-start.9
  646.9 54.7 %copy-start.19 = (bf16[192,768]{1,0:T(8,128)(2,1)S(1)}, bf16[192,768]{1,0:T(8,128)(2,1)}, u32[]{:S(2)}) copy-start(bf16[192,768]{1,0:T(8,128)(2,1)} %param.29) | copy-start | bytes 884740
  647.0 57.3 %copy-start.30 = (f32[384]{0:T(512)}, f32[384]{0:T(512)S(1)}, u32[]{:S(2)}) copy-start(f32[384]{0:T(512)S(1)} %broadcast_multiply_fusion.2) | copy-start | bytes 4612
  647.0 57.3 %copy-start.31 = (f32[384]{0:T(512)}, f32[384]{0:T(512)S(1)}, u32[]{:S(2)}) copy-start(f32[384]{0:T(512)S(1)} %broadcast_multiply_fusion.3) | copy-start | bytes 4612
  651.0 250.5 %reduce-scatter.21.cloned.1.call-start = ((), (), s32[]{:S(2)}) async-start(), calls=%async_computation.17 | async-start | bytes 884736
  781.8 9.8 copy-start.11
  781.8 9.8 copy-start.13
  781.8 5.8 copy-start.17
  793.6 7.8 copy-start.4
  797.5 105.6 %reduce-scatter.19.cloned.1.call-start = ((), (), s32[]{:S(2)}) async-start(), calls=%async_computation.16 | async-start | bytes 2211840
  809.9 5.1 copy-start.20
  814.7 5.0 copy-start.28
  814.7 111.3 %reduce-scatter.13.cloned.1.call-start = ((), (), s32[]{:S(2)}) async-start(), calls=%async_computation.12 | async-start | bytes 2949120 | tf_op jit(solution)/shard_map/reduce_scatter | solution.py:253
  819.6 171.9 %all-reduce.10.cloned.1.call-start = ((), (), s32[]{:S(2)}) async-start(), calls=%async_computation.15 | async-start | bytes 4718592 | tf_op jit(solution)/shard_map/psum | solution.py:280
  821.7 215.5 %reduce-scatter.15.cloned.1.call-start = ((), (), s32[]{:S(2)}) async-start(), calls=%async_computation.13 | async-start | bytes 2654208 | tf_op jit(solution)/shard_map/reduce_scatter | solution.py:266
  828.4 6.0 copy-start.24
  828.4 47.6 %copy-start.14 = (bf16[3,512,192]{1,2,0:T(8,128)(2,1)S(1)}, bf16[3,512,192]{1,2,0:T(8,128)(2,1)}, u32[]{:S(2)}) copy-start(bf16[3,512,192]{1,2,0:T(8,128)(2,1)} %copy-done.13) | copy-start | bytes 1769476
  828.4 254.9 %reduce-scatter.17.cloned.1.call-start = ((), (), s32[]{:S(2)}) async-start(), calls=%async_computation.14 | async-start | bytes 2654208 | tf_op jit(solution)/shard_map/reduce_scatter | solution.py:267
  834.4 41.7 %copy-start.12 = (bf16[3,512,192]{1,2,0:T(8,128)(2,1)S(1)}, bf16[3,512,192]{1,2,0:T(8,128)(2,1)}, u32[]{:S(2)}) copy-start(bf16[3,512,192]{1,2,0:T(8,128)(2,1)} %copy-done.11) | copy-start | bytes 1769476
  834.4 91.7 %copy-start.10 = (f32[384,768]{1,0:T(8,128)S(1)}, f32[384,768]{1,0:T(8,128)}, u32[]{:S(2)}) copy-start(f32[384,768]{1,0:T(8,128)} %copy-done.9) | copy-start | bytes 3538948
Sparse Core Ops, SparseCore 0:
  9.6 52.6 all-gather.3
  94.7 170.7 all-reduce.5
  291.2 170.9 all-reduce.7
  495.7 48.3 all-gather.5
  558.7 84.0 reduce-scatter.10
  651.1 50.4 all-gather.7
  797.7 33.6 reduce-scatter.20
  834.8 40.5 reduce-scatter.18
  878.3 47.6 reduce-scatter.12
  929.2 62.3 all-reduce.9
  995.5 41.6 reduce-scatter.14
  1041.0 42.3 reduce-scatter.16
where the time goes:
time: 1100 us; the launch traced here: 1090 us
  waiting for transfers between devices  753 us (68%)
  matrix products  137 us (12%)
  blocking collectives  81.6 us (7%)
  local copies, waits for them, and re-layouts  73.4 us (7%)
  other arithmetic  31 us (3%)
  between operations  15 us (1%)
    psum x1, waiting for transfers between devices, body(): lax.psum(jnp.dot(active, down_weight, preferred_element_type=jnp.float32)...  171 us
    psum x1, waiting for transfers between devices, body(): lax.psum(jnp.dot(context, out_weight, preferred_element_type=jnp.float32)...  171 us
    reduce_scatter x1, waiting for transfers between devices, body(): lax.psum_scatter(jnp.einsum('tf,df->td', grad_up, up_weight, preferred_el...  83.4 us
    psum x1, waiting for transfers between devices, body(): lax.psum((qv_bias_grad, up_bias_grad, pool_weight_grad, pool_bias_grad, c...  62.9 us
    all_gather x1, waiting for transfers between devices, body(): gathered = lax.all_gather(inputs, 'tensor', axis=0, tiled=True)  53.6 us
    all_gather x1, waiting for transfers between devices, body(): grad_att_all = lax.all_gather(grad_att, 'tensor', axis=0, tiled=True)  50.4 us
    all_gather x1, waiting for transfers between devices, body(): grad_fed_all = lax.all_gather(grad_fed, 'tensor', axis=0, tiled=True)  47.9 us
    reduce_scatter x1, waiting for transfers between devices, body(): lax.psum_scatter(down_weight_grad, 'dp', scatter_dimension=1, tiled=True)  46.2 us
  transfers between devices with their start and end apart: 12, of which 10 were waited for; matrix products, arithmetic and copies ran while one was open for 4% of the time, Pallas kernels for 0%

commit v1 on v0

--- a/solution.py
+++ b/solution.py
@@ -215,7 +215,17 @@
     )
     grad_att = grad_res.astype(jnp.bfloat16)
     out_bias_grad = jnp.sum(grad_att.astype(jnp.float32), axis=0)
-    grad_att_all = lax.all_gather(grad_att, "tensor", axis=0, tiled=True)
+    fresh = lax.axis_size("tensor")
+    d_next = lax.axis_index("tensor")
+    ready, new, z2 = (fresh, d_next, grad_att.shape[0])
+    panels = [(no, (no + 1) % ready) for no in range(ready)]
+    grad_att_all = jnp.zeros((*grad_att.shape[:0], ready * z2, *grad_att.shape[1:]), grad_att.dtype)
+    high = grad_att
+    for s in tuple(range(ready)):
+        h_now = (new - s) % ready
+        grad_att_all = lax.dynamic_update_slice_in_dim(grad_att_all, high, h_now * z2, axis=0)
+        if s < ready - 1:
+            high = lax.ppermute(high, "tensor", panels)
     out_weight_grad = jnp.einsum(
         "te,td->ed", context, grad_att_all, preferred_element_type=jnp.float32
     )

time: 1100 us -> 1100 us (level)
    all_gather x1 -> x0, waiting for transfers between devices: 50.4 us -> none  [body(): grad_att_all = lax.all_gather(grad_att, 'tensor', axis=0, tiled=True)]
    ppermute x0 -> x3, waiting for transfers between devices: none -> 45.9 us  [body(): high = lax.ppermute(high, 'tensor', panels)]
    unnamed x98 -> x100, local copies, waits for them, and re-layouts: 28.1 us -> 28.3 us
  transfers between devices with their start and end apart: 12 -> 14, of which waited for: 10 -> 12; matrix products, arithmetic and copies ran while one was open for 4% -> 4% of each run, Pallas kernels for 0% -> 0%
where the time goes in v1:
time: 1100 us; the launch traced here: 1090 us
  waiting for transfers between devices  750 us (68%)
  matrix products  134 us (12%)
  blocking collectives  80 us (7%)
  local copies, waits for them, and re-layouts  77 us (7%)
  other arithmetic  30.2 us (3%)
  between operations  14.7 us (1%)
    psum x1, waiting for transfers between devices, body(): lax.psum(jnp.dot(active, down_weight, preferred_element_type=jnp.float32)...  171 us
    psum x1, waiting for transfers between devices, body(): lax.psum(jnp.dot(context, out_weight, preferred_element_type=jnp.float32)...  171 us
    reduce_scatter x1, waiting for transfers between devices, body(): lax.psum_scatter(jnp.einsum('tf,df->td', grad_up, up_weight, preferred_el...  83.4 us
    psum x1, waiting for transfers between devices, body(): lax.psum((qv_bias_grad, up_bias_grad, pool_weight_grad, pool_bias_grad, c...  63 us
    all_gather x1, waiting for transfers between devices, body(): gathered = lax.all_gather(inputs, 'tensor', axis=0, tiled=True)  53.6 us
    all_gather x1, waiting for transfers between devices, body(): grad_fed_all = lax.all_gather(grad_fed, 'tensor', axis=0, tiled=True)  48.2 us
    reduce_scatter x1, waiting for transfers between devices, body(): lax.psum_scatter(down_weight_grad, 'dp', scatter_dimension=1, tiled=True)  46.3 us
    ppermute x3, waiting for transfers between devices, body(): high = lax.ppermute(high, 'tensor', panels)  45.9 us
  transfers between devices with their start and end apart: 14, of which 12 were waited for; matrix products, arithmetic and copies ran while one was open for 4% of the time, Pallas kernels for 0%

profile of v1, /device:TPU:0, one launch (start us, length us, event | category | flops | bytes accessed | tf_op | source)
XLA Modules:
  0.0 1089.1 jit_solution(9138317968665860672)
XLA Ops:
  8.8 53.6 %all-gather.3.cloned.1.call-done = bf16[1536,768]{1,0:T(8,128)(2,1)} async-done(((bf16[384,768]{1,0:T(8,128)(2,1)}), bf16[1536,768]{1,0:T(8,128)(2,1)}) %all-gather.3.cloned.1.call-update) | async-done | bytes 2359312 | tf_op jit(solution)/shard_map/all_gather | solution.py:120
  62.3 3.5 convolution_bitcast_fusion
  68.3 1.9 squeeze.20
  70.7 1.9 squeeze.21
  73.1 2.1 convert_element_type.164
  76.6 12.6 %while.26 = (s32[]{:T(128)}, bf16[3,512,192]{1,2,0:T(8,128)(2,1)S(1)}, f32[3,3,512]{2,1,0:T(4,128)}, bf16[3,512,192]{1,2,0:T(8,128)(2,1)S(1)}, s32[3,512]{1,0:T(...) while((s32[]{:T(128)}, bf16[3,512,192]{1,2,0:T(8,128)(2,1)S(1)}, ...), condition=%wide.region_3.4_spmd, body=%wide.region_0.3_spmd.sunk | while | flops 211122688 | bytes 12902513 | solution.py:131
  90.6 4.0 fusion.92
  94.8 170.7 %all-reduce.6.cloned.1.call-done = f32[1536,768]{1,0:T(8,128)} async-done(((f32[1536,768]{1,0:T(8,128)}), f32[1536,768]{1,0:T(8,128)}) %all-reduce.6.cloned.1.call-update) | async-done | bytes 4718608 | tf_op jit(solution)/shard_map/psum | solution.py:137
  265.4 3.2 fusion.52
  272.2 13.3 %multiply_convert_fusion = (bf16[1536,768]{1,0:T(8,128)(2,1)S(1)}, f32[1536,768]{1,0:T(8,128)}, f32[1536,768]{1,0:T(8,128)}) fusion(f32[768]{0:T(1024)S(1)} %copy-done.41, bf16[768,768]{1,0:T(8,128)(2,1)S(1)} %copy-done, f32[1536,768]{1,0:T(8,128)S(1)} %subtract_multiply_fusion.1, f32[768]{0:T(1024)S(1)} %copy-done.36, f32[768]{0:T(1024)S(1)} %copy-done.23), kind=kOutput, calls=%fused_computation.53 | convolution fusion | flops 1893335040 | bytes 17703936 | tf_op jit(solution)/shard_map/dot_general | solution.py:146
  286.9 4.2 fusion.93
  291.2 171.0 %all-reduce.8.cloned.1.call-done = f32[1536,768]{1,0:T(8,128)} async-done(((f32[1536,768]{1,0:T(8,128)}), f32[1536,768]{1,0:T(8,128)}) %all-reduce.8.cloned.1.call-update) | async-done | bytes 4718608 | tf_op jit(solution)/shard_map/psum | solution.py:150
  462.2 4.7 fusion.86
  468.3 2.0 copy-done.5
  470.9 16.4 %psum.107 = bf16[3,768]{1,0:T(4,128)(2,1)S(1)} all-reduce(f32[3,768]{1,0:T(4,128)S(1)} %fusion.56), channel_id=1, replica_groups=mesh['dp'=8,'tensor'=4] {'tensor'}, use_global_device_ids=true, to_apply=%region_10.11 | all-reduce | flops 2304 | bytes 13824 | tf_op jit(solution)/shard_map/psum | solution.py:163
  489.6 3.0 multiply_reduce_fusion.3
  492.6 3.0 convert_reduce_fusion.1
  495.9 48.2 %all-gather.5.cloned.1.call-done = bf16[1536,768]{1,0:T(8,128)(2,1)} async-done(((bf16[384,768]{1,0:T(8,128)(2,1)}), bf16[1536,768]{1,0:T(8,128)(2,1)}) %all-gather.5.cloned.1.call-update) | async-done | bytes 2359312 | tf_op jit(solution)/shard_map/all_gather | solution.py:194
  544.1 8.8 convert_reduce_fusion
  554.3 4.3 fusion.95
  559.5 83.4 %reduce-scatter.11.cloned.1.call-done = f32[384,768]{1,0:T(8,128)} async-done(((f32[1536,768]{1,0:T(8,128)}), f32[384,768]{1,0:T(8,128)}) %reduce-scatter.11.cloned.1.call-update) | async-done | bytes 1179664 | tf_op jit(solution)/shard_map/reduce_scatter | solution.py:205
  642.9 4.1 multiply_reduce_fusion.4
  648.0 2.2 convert_reduce_fusion.2
  651.7 15.3 %collective-permute-done = bf16[384,768]{1,0:T(8,128)(2,1)S(1)} collective-permute-done((bf16[384,768]{1,0:T(8,128)(2,1)S(1)}, bf16[384,768]{1,0:T(8,128)(2,1)S(1)}, u32[]{:S(2)}, u32[]{:S(2)}) %collective-permute-start) | collective-permute-done | bytes 589856 | tf_op jit(solution)/shard_map/ppermute | solution.py:228
  667.0 15.9 %collective-permute-done.1 = bf16[384,768]{1,0:T(8,128)(2,1)S(1)} collective-permute-done((bf16[384,768]{1,0:T(8,128)(2,1)S(1)}, bf16[384,768]{1,0:T(8,128)(2,1)S(1)}, u32[]{:S(2)}, u32[]{:S(2)}) %collective-permute-start.1) | collective-permute-done | bytes 589856 | tf_op jit(solution)/shard_map/ppermute | solution.py:228
  683.8 14.7 %collective-permute-done.2 = bf16[384,768]{1,0:T(8,128)(2,1)S(1)} collective-permute-done((bf16[384,768]{1,0:T(8,128)(2,1)S(1)}, bf16[384,768]{1,0:T(8,128)(2,1)S(1)}, u32[]{:S(2)}, u32[]{:S(2)}) %collective-permute-start.2) | collective-permute-done | bytes 589856 | tf_op jit(solution)/shard_map/ppermute | solution.py:228
  699.5 2.0 convolution_bitcast_fusion.1
  703.4 75.7 %while.27 = (s32[]{:T(128)}, bf16[3,512,192]{1,2,0:T(8,128)(2,1)S(1)}, bf16[3,512,192]{1,2,0:T(8,128)(2,1)}, bf16[3,512,192]{1,2,0:T(8,128)(2,1)S(1)}, bf16[3,51...) while((s32[]{:T(128)}, ...), condition=%wide.region_20.21_spmd, body=%wide.region_18.20_spmd.sunk | while | flops 515084288 | bytes 27811988 | solution.py:235
  706.9 2.6 subtract_exponential_fusion.4
  711.4 2.4 fusion.175
  713.8 5.8 fusion.176
  719.6 2.5 fusion.177
  722.1 5.8 fusion.178
  732.1 2.6 subtract_exponential_fusion.4
  736.6 2.4 fusion.175
  739.0 5.8 fusion.176
  744.8 2.5 fusion.177
  747.3 5.8 fusion.178
  757.4 2.6 subtract_exponential_fusion.4
  761.9 2.4 fusion.175
  764.2 5.8 fusion.176
  770.0 2.5 fusion.177
  772.5 5.8 fusion.178
  780.5 2.5 stack_reshape.9
  783.0 1.9 constant_dynamic-update-slice_fusion.6
  786.3 2.5 stack_reshape.10
  788.8 2.6 copy.81
  791.4 2.5 stack_reshape.11
  794.0 1.9 constant_dynamic-update-slice_fusion.5
  797.8 4.3 fusion.49
  802.1 4.2 copy.87
  806.3 4.8 reshape.315
  811.4 4.7 bitcast_convert_fusion
  816.2 2.0 fusion.97
  818.2 6.6 fusion.58
  824.9 6.0 fusion.96
  832.5 38.8 %all-reduce = (f32[768]{0:T(1024)}, f32[768]{0:T(1024)}, f32[768]{0:T(1024)}, f32[768]{0:T(1024)}, f32[768]{0:T(1024)}, /*index=5*/f32[768]{0:T(1024)}) all-reduce(f32[768]{0:T(1024)} %get-tuple-element.275, f32[768]{0:T(1024)} %get-tuple-element.222, ...), channel_id=1, replica_groups=mesh['dp'=8,'tensor'=4] {'dp','tensor'}, use_global_device_ids=true, to_apply=%region_28.29 | all-reduce | flops 4608 | bytes 36864 | tf_op jit(solution)/shard_map/psum | solution.py:279
  871.6 24.8 %all-reduce.1 = (f32[2,192]{1,0:T(2,128)}, f32[768]{0:T(1024)}, f32[768]{0:T(1024)}, f32[768,3]{0,1:T(4,128)}, f32[3]{0:T(128)}) all-reduce(f32[2,192]{1,0:T(2,128)S(1)} %pad_maximum_fusion, f32[768]{0:T(1024)} %get-tuple-element.279, f32[768]{0:T(1024)} %get-tuple-element.301, ...), channel_id=1, replica_groups=mesh['dp'=8,'tensor'=4] {'dp'}, use_global_device_ids=true, to_apply=%region_25.26 | all-reduce | flops 4227 | bytes 33816 | tf_op jit(solution)/shard_map/psum | solution.py:290
  899.9 21.8 %reduce-scatter.13.cloned.1.call-done = bf16[384,768]{1,0:T(8,128)(2,1)} async-done(((bf16[1536,768]{1,0:T(8,128)(2,1)}), bf16[384,768]{1,0:T(8,128)(2,1)}) %reduce-scatter.13.cloned.1.call-update) | async-done | bytes 589840 | tf_op jit(solution)/shard_map/reduce_scatter | solution.py:263
  921.7 2.6 add_convert_fusion.3
  924.4 63.0 %all-reduce.10.cloned.1.call-done = f32[768,768]{1,0:T(8,128)} async-done(((f32[768,768]{1,0:T(8,128)}), f32[768,768]{1,0:T(8,128)}) %all-reduce.10.cloned.1.call-update) | async-done | bytes 2359312 | tf_op jit(solution)/shard_map/psum | solution.py:290
  987.4 45.5 %reduce-scatter.15.cloned.1.call-done = f32[96,768]{1,0:T(8,128)} async-done(((f32[768,768]{1,0:T(8,128)}), f32[96,768]{1,0:T(8,128)}) %reduce-scatter.15.cloned.1.call-update) | async-done | bytes 294928 | tf_op jit(solution)/shard_map/reduce_scatter | solution.py:276
  1032.9 46.3 %reduce-scatter.17.cloned.1.call-done = f32[768,96]{0,1:T(8,128)} async-done(((f32[768,768]{0,1:T(8,128)}), f32[768,96]{0,1:T(8,128)}) %reduce-scatter.17.cloned.1.call-update) | async-done | bytes 294928 | tf_op jit(solution)/shard_map/reduce_scatter | solution.py:277
  1079.2 3.2 copy.133
  (225 shorter events, 67.0 us)
Async XLA Ops:
  7.2 265.0 %copy-start = (bf16[768,768]{1,0:T(8,128)(2,1)S(1)}, bf16[768,768]{1,0:T(8,128)(2,1)}, u32[]{:S(2)}) copy-start(bf16[768,768]{1,0:T(8,128)(2,1)} %param.33) | copy-start | bytes 3538948
  7.2 55.1 %all-gather.3.cloned.1.call-start = ((), (), s32[]{:S(2)}) async-start(), calls=%async_computation.6 | async-start | bytes 2949120 | tf_op jit(solution)/shard_map/all_gather | solution.py:120
  7.9 257.5 %all-reduce.6.cloned.1.call-start = ((), (), s32[]{:S(2)}) async-start(), calls=%async_computation.7 | async-start | bytes 9437184 | tf_op jit(solution)/shard_map/psum | solution.py:137
  89.2 0.8 copy-start.6
  89.2 1.0 copy-start.7
  89.2 1.2 copy-start.8
  89.2 1.4 copy-start.15
  94.5 170.9 %copy-start.3 = (bf16[1536,768]{1,0:T(8,128)(2,1)S(1)}, bf16[1536,768]{1,0:T(8,128)(2,1)}, u32[]{:S(2)}) copy-start(bf16[1536,768]{1,0:T(8,128)(2,1)} %all-gather.3.cloned.1.call-done) | copy-start | bytes 7077892
  94.5 170.9 %copy-start.27 = (f32[768]{0:T(1024)S(1)}, f32[768]{0:T(1024)}, u32[]{:S(2)}) copy-start(f32[768]{0:T(1024)} %param.30) | copy-start | bytes 9220
  94.6 367.7 %all-reduce.8.cloned.1.call-start = ((), (), s32[]{:S(2)}) async-start(), calls=%async_computation.8 | async-start | bytes 9437184 | tf_op jit(solution)/shard_map/psum | solution.py:150
  265.4 3.8 copy-start.1
  270.4 0.6 copy-start.26
  271.0 1.2 copy-start.23
  271.0 1.2 copy-start.36
  271.0 1.2 copy-start.41
  272.2 13.3 %copy-start.2 = (f32[1536,768]{1,0:T(8,128)}, f32[1536,768]{1,0:T(8,128)S(1)}, u32[]{:S(2)}) copy-start(f32[1536,768]{1,0:T(8,128)S(1)} %subtract_multiply_fusion.1) | copy-start | bytes 14155780
  272.2 14.7 %copy-start.39 = (bf16[768,768]{1,0:T(8,128)(2,1)S(1)}, bf16[768,768]{1,0:T(8,128)(2,1)}, u32[]{:S(2)}) copy-start(bf16[768,768]{1,0:T(8,128)(2,1)} %param.35) | copy-start | bytes 3538948
  285.5 1.4 copy-start.44
  291.1 171.1 %copy-start.34 = (f32[768]{0:T(1024)S(1)}, f32[768]{0:T(1024)}, u32[]{:S(2)}) copy-start(f32[768]{0:T(1024)} %param.36) | copy-start | bytes 9220
  291.2 253.0 %all-gather.5.cloned.1.call-start = ((), (), s32[]{:S(2)}) async-start(), calls=%async_computation.9 | async-start | bytes 2949120 | tf_op jit(solution)/shard_map/all_gather | solution.py:194
  467.6 2.7 copy-start.22
  467.6 2.7 copy-start.33
  467.6 19.7 %copy-start.17 = (bf16[768,768]{1,0:T(8,128)(2,1)S(1)}, bf16[768,768]{1,0:T(8,128)(2,1)}, u32[]{:S(2)}) copy-start(bf16[768,768]{1,0:T(8,128)(2,1)} %param.39) | copy-start | bytes 3538948
  467.6 19.7 %copy-start.35 = (f32[768]{0:T(1024)S(1)}, f32[768]{0:T(1024)}, u32[]{:S(2)}) copy-start(f32[768]{0:T(1024)} %param.40) | copy-start | bytes 9220
  467.6 19.9 %copy-start.40 = (bf16[768,3]{0,1:T(4,128)(2,1)S(1)}, bf16[768,3]{0,1:T(4,128)(2,1)}, u32[]{:S(2)}) copy-start(bf16[768,3]{0,1:T(4,128)(2,1)} %param.41) | copy-start | bytes 13828
  467.6 19.9 %copy-start.43 = (f32[3]{0:T(128)S(1)}, f32[3]{0:T(128)}, u32[]{:S(2)}) copy-start(f32[3]{0:T(128)} %param.42) | copy-start | bytes 40
  467.7 20.1 %copy-start.38 = (s32[3]{0:T(128)S(1)}, s32[3]{0:T(128)}, u32[]{:S(2)}) copy-start(s32[3]{0:T(128)} %param.26) | copy-start | bytes 40
  468.2 2.1 copy-start.5
  468.2 21.4 %copy-start.19 = (bf16[384,768]{1,0:T(8,128)(2,1)S(1)}, bf16[384,768]{1,0:T(8,128)(2,1)}, u32[]{:S(2)}) copy-start(bf16[384,768]{1,0:T(8,128)(2,1)} %param.43) | copy-start | bytes 1769476
  487.6 1.6 copy-start.24
  488.4 0.8 copy-start.37
  489.2 6.4 copy-start.28
  489.6 54.5 %copy-start.42 = (f32[768]{0:T(1024)S(1)}, f32[768]{0:T(1024)}, u32[]{:S(2)}) copy-start(f32[768]{0:T(1024)} %param.34) | copy-start | bytes 9220
  495.6 147.2 %reduce-scatter.11.cloned.1.call-start = ((), (), s32[]{:S(2)}) async-start(), calls=%async_computation.10 | async-start | bytes 5898240 | tf_op jit(solution)/shard_map/reduce_scatter | solution.py:205
  552.9 1.4 copy-start.45
  558.7 337.7 %reduce-scatter.21.cloned.1.call-start = ((), (), s32[]{:S(2)}) async-start(), calls=%async_computation.16 | async-start | bytes 884736
  559.5 87.5 %copy-start.30 = (f32[384]{0:T(512)}, f32[384]{0:T(512)S(1)}, u32[]{:S(2)}) copy-start(f32[384]{0:T(512)S(1)} %dynamic-slice.6) | copy-start | bytes 4612
  647.0 1.0 copy-start.9
  647.0 20.0 %copy-start.31 = (f32[384]{0:T(512)}, f32[384]{0:T(512)S(1)}, u32[]{:S(2)}) copy-start(f32[384]{0:T(512)S(1)} %broadcast_multiply_fusion.2) | copy-start | bytes 4612
  647.0 20.0 %copy-start.32 = (f32[384]{0:T(512)}, f32[384]{0:T(512)S(1)}, u32[]{:S(2)}) copy-start(f32[384]{0:T(512)S(1)} %broadcast_multiply_fusion.3) | copy-start | bytes 4612
  650.2 16.8 %collective-permute-start = (bf16[384,768]{1,0:T(8,128)(2,1)S(1)}, bf16[384,768]{1,0:T(8,128)(2,1)S(1)}, u32[]{:S(2)}, u32[]{:S(2)}) collective-permute-start(bf16[384,768]{1,0:T(8,128)(2,1)S(1)} %get-tuple-element.276), channel_id=1, source_target_pairs={{0,1},{1,2},{2,3},{3,0},{4,5},{5,6},{6,7},{7,4},{8,9},{9,10},{10,1... | collective-permute-start | bytes 1769480 | tf_op jit(solution)/shard_map/ppermute | solution.py:228
  667.0 16.0 %collective-permute-start.1 = (bf16[384,768]{1,0:T(8,128)(2,1)S(1)}, bf16[384,768]{1,0:T(8,128)(2,1)S(1)}, u32[]{:S(2)}, u32[]{:S(2)}) collective-permute-start(bf16[384,768]{1,0:T(8,128)(2,1)S(1)} %collective-permute-done), channel_id=1, source_target_pairs={{0,1},{1,2},{2,3},{3,0},{4,5},{5,6},{6,7},{7,4},{8,9},{9,10},{10,1... | collective-permute-start | bytes 1769480 | tf_op jit(solution)/shard_map/ppermute | solution.py:228
  682.9 15.5 %collective-permute-start.2 = (bf16[384,768]{1,0:T(8,128)(2,1)S(1)}, bf16[384,768]{1,0:T(8,128)(2,1)S(1)}, u32[]{:S(2)}, u32[]{:S(2)}) collective-permute-start(bf16[384,768]{1,0:T(8,128)(2,1)S(1)} %collective-permute-done.1), channel_id=1, source_target_pairs={{0,1},{1,2},{2,3},{3,0},{4,5},{5,6},{6,7},{7,4},{8,9},{9,10},{10,1... | collective-permute-start | bytes 1769480 | tf_op jit(solution)/shard_map/ppermute | solution.py:228
  683.4 15.1 %copy-start.20 = (bf16[192,768]{1,0:T(8,128)(2,1)S(1)}, bf16[192,768]{1,0:T(8,128)(2,1)}, u32[]{:S(2)}) copy-start(bf16[192,768]{1,0:T(8,128)(2,1)} %param.29) | copy-start | bytes 884740
  698.5 1.1 copy-start.16
  779.1 7.2 copy-start.11
  779.1 7.2 copy-start.13
  779.1 5.8 copy-start.18
  788.8 9.0 copy-start.4
  793.9 104.1 %reduce-scatter.19.cloned.1.call-start = ((), (), s32[]{:S(2)}) async-start(), calls=%async_computation.15 | async-start | bytes 2211840
  806.3 5.0 copy-start.21
  811.1 5.0 copy-start.29
  811.2 110.6 %reduce-scatter.13.cloned.1.call-start = ((), (), s32[]{:S(2)}) async-start(), calls=%async_computation.11 | async-start | bytes 2949120 | tf_op jit(solution)/shard_map/reduce_scatter | solution.py:263
  816.1 171.3 %all-reduce.10.cloned.1.call-start = ((), (), s32[]{:S(2)}) async-start(), calls=%async_computation.14 | async-start | bytes 4718592 | tf_op jit(solution)/shard_map/psum | solution.py:290
  818.2 214.7 %reduce-scatter.15.cloned.1.call-start = ((), (), s32[]{:S(2)}) async-start(), calls=%async_computation.12 | async-start | bytes 2654208 | tf_op jit(solution)/shard_map/reduce_scatter | solution.py:276
  824.9 6.1 copy-start.25
  824.9 46.4 %copy-start.14 = (bf16[3,512,192]{1,2,0:T(8,128)(2,1)S(1)}, bf16[3,512,192]{1,2,0:T(8,128)(2,1)}, u32[]{:S(2)}) copy-start(bf16[3,512,192]{1,2,0:T(8,128)(2,1)} %copy-done.13) | copy-start | bytes 1769476
  824.9 254.3 %reduce-scatter.17.cloned.1.call-start = ((), (), s32[]{:S(2)}) async-start(), calls=%async_computation.13 | async-start | bytes 2654208 | tf_op jit(solution)/shard_map/reduce_scatter | solution.py:277
  830.9 40.5 %copy-start.12 = (bf16[3,512,192]{1,2,0:T(8,128)(2,1)S(1)}, bf16[3,512,192]{1,2,0:T(8,128)(2,1)}, u32[]{:S(2)}) copy-start(bf16[3,512,192]{1,2,0:T(8,128)(2,1)} %copy-done.11) | copy-start | bytes 1769476
  830.9 90.8 %copy-start.10 = (f32[384,768]{1,0:T(8,128)S(1)}, f32[384,768]{1,0:T(8,128)}, u32[]{:S(2)}) copy-start(f32[384,768]{1,0:T(8,128)} %copy-done.9) | copy-start | bytes 3538948
Sparse Core Ops, SparseCore 0:
  9.6 52.6 all-gather.2
  94.7 170.7 all-reduce.5
  291.3 170.9 all-reduce.7
  495.8 48.3 all-gather.4
  558.8 84.0 reduce-scatter.10
  794.1 33.0 reduce-scatter.20
  830.6 40.6 reduce-scatter.18
  874.1 47.5 reduce-scatter.12
  925.0 62.3 all-reduce.9
  991.2 41.6 reduce-scatter.14
  1036.8 42.3 reduce-scatter.16
